TPU v7x, 32 devices: a whole 2x2x4 slice. The times are simulated.
32 devices in a mesh: dp: 8 (over z, core), ctx: 4 (over y, x).
Axes of the slice: x: 2, y: 2, z: 4, core: 2. Of those that a mesh axis runs over, the one named last changes fastest.
Arguments:
- state_rows: bfloat16 [12288, 2048], P(('dp', 'ctx')), parts along dimension 0, may hold values from -6 to 6
- query_vectors: bfloat16 [8, 12288, 128], P(None, ('dp', 'ctx')), parts along dimension 1, may hold values from -6 to 6
- key_vectors: bfloat16 [8, 12288, 128], P(None, ('dp', 'ctx')), parts along dimension 1, may hold values from -6 to 6
- value_vectors: bfloat16 [8, 12288, 128], P(None, ('dp', 'ctx')), parts along dimension 1, may hold values from -24 to 24
- halt_counts: int32 [12288], P(('dp', 'ctx')), parts along dimension 0, may hold values from 1 to 6, as said below
- out_weight: bfloat16 [8, 128, 2048], replicated, may hold values from -0.75 to 0.75
- norm_gain: bfloat16 [2048], replicated, may hold values from 0.099609375 to 1.8984375
Outputs:
- new_state: bfloat16 [12288, 2048], P(('dp', 'ctx')), parts along dimension 0
There are 8 independent parts, one for each index of `dp`. A program takes and returns all parts, laid end to end along the dimension named above; an argument that names none is the same for every part. Nothing has to cross between parts.
Inputs may be any that keep to these rules, and one draw needn't show every extreme that they name: halt_counts is equal within each aligned tile of 128 positions; exactly 3 tiles of a document have counts above 2, and on some device of ctx all 3 tiles do.
All inputs are finite; a program needn't handle non-finite values.
Results may differ from a plain program's by a relative error of at most 0.008.
Values may be sent and summed in bfloat16 or wider, within the bound.
A program may use at most 128 MiB of HBM per device.

v0:
```python
import jax
import jax.numpy as jnp
from jax import lax
from jax.sharding import PartitionSpec as P

STEP = 2


def fold_heads(carry, queries, key_piece, value_piece, score_scale):
    running_max, running_sum, weighted = carry

    def per_head(head_items):
        query_head, key_head, value_head, max_head, sum_head, weighted_head = head_items
        scores = (
            lax.dot_general(
                query_head, key_head, (((1,), (1,)), ((), ())), preferred_element_type=jnp.float32
            )
            * score_scale
        )
        new_max = jnp.maximum(max_head, jnp.max(scores, axis=1))
        shrink = jnp.exp(max_head - new_max)
        exponents = jnp.exp(scores - new_max[:, None])
        sum_head = sum_head * shrink + jnp.sum(exponents, axis=1)
        weighted_head = weighted_head * shrink[:, None] + jnp.dot(
            exponents.astype(jnp.bfloat16), value_head, preferred_element_type=jnp.float32
        )
        return (new_max, sum_head, weighted_head)

    return lax.map(per_head, (queries, key_piece, value_piece, running_max, running_sum, weighted))


def empty_carry(head_count, query_count, head_width):
    return (
        jnp.full((head_count, query_count), -1e30, jnp.float32),
        jnp.zeros((head_count, query_count), jnp.float32),
        jnp.zeros((head_count, query_count, head_width), jnp.float32),
    )


def attend_keys(query_vectors, key_vectors, value_vectors, score_scale):
    head_count, row_count, head_width = query_vectors.shape
    initial = empty_carry(head_count, row_count, head_width)
    running_max, running_sum, weighted = fold_heads(
        initial,
        query_vectors,
        lax.all_gather(key_vectors, "ctx", axis=1, tiled=True),
        lax.all_gather(value_vectors, "ctx", axis=1, tiled=True),
        score_scale,
    )
    return (weighted / running_sum[..., None]).astype(jnp.bfloat16)


def on_device(
    state_rows, query_vectors, key_vectors, value_vectors, halt_counts, out_weight, norm_gain
):
    head_count, row_count, head_width = query_vectors.shape
    score_scale = head_width ** (-0.5)
    attended = attend_keys(query_vectors, key_vectors, value_vectors, score_scale)
    update = jnp.einsum("hqd,hde->qe", attended, out_weight, preferred_element_type=jnp.float32)
    mixed_sum = state_rows.astype(jnp.float32) + update
    normed = (
        mixed_sum
        * lax.rsqrt(jnp.mean(mixed_sum * mixed_sum, axis=-1, keepdims=True) + 1e-06)
        * norm_gain.astype(jnp.float32)
    )
    active = (halt_counts > STEP)[:, None]
    return jnp.where(active, normed.astype(jnp.bfloat16), state_rows)


def solution(mesh):
    placed = (
        P(("dp", "ctx"), None),
        P(None, ("dp", "ctx"), None),
        P(None, ("dp", "ctx"), None),
        P(None, ("dp", "ctx"), None),
        P(("dp", "ctx")),
        P(),
        P(),
    )
    return jax.shard_map(
        on_device, mesh=mesh, in_specs=placed, out_specs=P(("dp", "ctx"), None), check_vma=False
    )
```

profile of v0, /device:TPU:0, one launch (start us, length us, event | category | flops | bytes accessed | tf_op | source)
XLA Modules:
  0.0 150.3 jit_solution(8866256472894087559)
XLA Ops:
  6.5 0.7 all-gather.3.cloned.1.call-update
  7.3 0.7 all-gather.5.cloned.1.call-update
  8.0 0.7 convert_element_type.17
  9.4 46.4 %all-gather.3.cloned.1.call-done = bf16[8,1536,128]{2,1,0:T(8,128)(2,1)} async-done(((bf16[8,384,128]{2,1,0:T(8,128)(2,1)}), bf16[8,1536,128]{2,1,0:T(8,128)(2,1)}) %all-gather.3.cloned.1.call-update) | async-done | bytes 3145744 | tf_op jit(solution)/shard_map/all_gather | solution.py:46
  55.8 45.7 %all-gather.5.cloned.1.call-done = bf16[8,1536,128]{2,1,0:T(8,128)(2,1)} async-done(((bf16[8,384,128]{2,1,0:T(8,128)(2,1)}), bf16[8,1536,128]{2,1,0:T(8,128)(2,1)}) %all-gather.5.cloned.1.call-update) | async-done | bytes 3145744 | tf_op jit(solution)/shard_map/all_gather | solution.py:47
  101.5 35.0 %while.12 = (s32[]{:T(128)}, f32[8,384]{1,0:T(8,128)S(1)}, f32[8,384,128]{2,1,0:T(8,128)}, bf16[8,384,128]{2,1,0:T(8,128)(2,1)}, bf16[8,1536,128]{2,1,0:T(8,128)...) while((s32[]{:T(128)}, f32[8,384]{1,0:T(8,128)S(1)}, f32[8,384,128]{2,1,0:T(8,128)}, ...), condition=%wide.region_3.4_spmd, body=%wide.region_0.3_spmd.sunk | while | flops 305579136 | bytes 8184417 | solution.py:29
  101.5 1.6 %fusion.34 = (f32[384]{0:T(512)S(1)}, f32[384,1536]{1,0:T(8,128)S(1)}) fusion(bf16[8,1536,128]{2,1,0:T(8,128)(2,1)} %get-tuple-element.123, s32[]{:T(128)S(6)} %copy.13, bf16[8,384,128]{2,1,0:T(8,128)(2,1)} %get-tuple-element.122), kind=kOutput, calls=%fused_computation.28.clone.1 | convolution fusion | flops 152174208 | bytes 2853376 | tf_op jit(solution)/shard_map/while/body/eval_jaxpr/dot_general | solution.py:15
  103.7 2.2 %fusion.36 = f32[8,384,128]{2,1,0:T(8,128)} fusion(f32[8,384,128]{2,1,0:T(8,128)} %get-tuple-element.113, s32[]{:T(128)S(6)} %copy.13, f32[384,1536]{1,0:T(8,128)S(1)} %get-tuple-element.100, f32[384]{0:T(512)S(1)} %broadcast_maximum_fusion.2, bf16[8,1536,128]{2,1,0:T(8,128)(2,1)} %get-tuple-element.124, f32[384]{0:T(512)S(1)} %get-tuple-element.102), kind=kOutput, calls=%fused_computation.8.clone.1 | convolution fusion | flops 152223744 | bytes 2953216 | tf_op jit(solution)/shard_map/while/body/eval_jaxpr/dot_general | solution.py:24
  105.9 1.6 %fusion.34 = (f32[384]{0:T(512)S(1)}, f32[384,1536]{1,0:T(8,128)S(1)}) fusion(bf16[8,1536,128]{2,1,0:T(8,128)(2,1)} %get-tuple-element.123, s32[]{:T(128)S(6)} %copy.13, bf16[8,384,128]{2,1,0:T(8,128)(2,1)} %get-tuple-element.122), kind=kOutput, calls=%fused_computation.28.clone.1 | convolution fusion | flops 152174208 | bytes 2853376 | tf_op jit(solution)/shard_map/while/body/eval_jaxpr/dot_general | solution.py:15
  108.0 2.2 %fusion.36 = f32[8,384,128]{2,1,0:T(8,128)} fusion(f32[8,384,128]{2,1,0:T(8,128)} %get-tuple-element.113, s32[]{:T(128)S(6)} %copy.13, f32[384,1536]{1,0:T(8,128)S(1)} %get-tuple-element.100, f32[384]{0:T(512)S(1)} %broadcast_maximum_fusion.2, bf16[8,1536,128]{2,1,0:T(8,128)(2,1)} %get-tuple-element.124, f32[384]{0:T(512)S(1)} %get-tuple-element.102), kind=kOutput, calls=%fused_computation.8.clone.1 | convolution fusion | flops 152223744 | bytes 2953216 | tf_op jit(solution)/shard_map/while/body/eval_jaxpr/dot_general | solution.py:24
  110.2 1.6 %fusion.34 = (f32[384]{0:T(512)S(1)}, f32[384,1536]{1,0:T(8,128)S(1)}) fusion(bf16[8,1536,128]{2,1,0:T(8,128)(2,1)} %get-tuple-element.123, s32[]{:T(128)S(6)} %copy.13, bf16[8,384,128]{2,1,0:T(8,128)(2,1)} %get-tuple-element.122), kind=kOutput, calls=%fused_computation.28.clone.1 | convolution fusion | flops 152174208 | bytes 2853376 | tf_op jit(solution)/shard_map/while/body/eval_jaxpr/dot_general | solution.py:15
  112.4 2.2 %fusion.36 = f32[8,384,128]{2,1,0:T(8,128)} fusion(f32[8,384,128]{2,1,0:T(8,128)} %get-tuple-element.113, s32[]{:T(128)S(6)} %copy.13, f32[384,1536]{1,0:T(8,128)S(1)} %get-tuple-element.100, f32[384]{0:T(512)S(1)} %broadcast_maximum_fusion.2, bf16[8,1536,128]{2,1,0:T(8,128)(2,1)} %get-tuple-element.124, f32[384]{0:T(512)S(1)} %get-tuple-element.102), kind=kOutput, calls=%fused_computation.8.clone.1 | convolution fusion | flops 152223744 | bytes 2953216 | tf_op jit(solution)/shard_map/while/body/eval_jaxpr/dot_general | solution.py:24
  114.6 1.6 %fusion.34 = (f32[384]{0:T(512)S(1)}, f32[384,1536]{1,0:T(8,128)S(1)}) fusion(bf16[8,1536,128]{2,1,0:T(8,128)(2,1)} %get-tuple-element.123, s32[]{:T(128)S(6)} %copy.13, bf16[8,384,128]{2,1,0:T(8,128)(2,1)} %get-tuple-element.122), kind=kOutput, calls=%fused_computation.28.clone.1 | convolution fusion | flops 152174208 | bytes 2853376 | tf_op jit(solution)/shard_map/while/body/eval_jaxpr/dot_general | solution.py:15
  116.8 2.2 %fusion.36 = f32[8,384,128]{2,1,0:T(8,128)} fusion(f32[8,384,128]{2,1,0:T(8,128)} %get-tuple-element.113, s32[]{:T(128)S(6)} %copy.13, f32[384,1536]{1,0:T(8,128)S(1)} %get-tuple-element.100, f32[384]{0:T(512)S(1)} %broadcast_maximum_fusion.2, bf16[8,1536,128]{2,1,0:T(8,128)(2,1)} %get-tuple-element.124, f32[384]{0:T(512)S(1)} %get-tuple-element.102), kind=kOutput, calls=%fused_computation.8.clone.1 | convolution fusion | flops 152223744 | bytes 2953216 | tf_op jit(solution)/shard_map/while/body/eval_jaxpr/dot_general | solution.py:24
  119.0 1.6 %fusion.34 = (f32[384]{0:T(512)S(1)}, f32[384,1536]{1,0:T(8,128)S(1)}) fusion(bf16[8,1536,128]{2,1,0:T(8,128)(2,1)} %get-tuple-element.123, s32[]{:T(128)S(6)} %copy.13, bf16[8,384,128]{2,1,0:T(8,128)(2,1)} %get-tuple-element.122), kind=kOutput, calls=%fused_computation.28.clone.1 | convolution fusion | flops 152174208 | bytes 2853376 | tf_op jit(solution)/shard_map/while/body/eval_jaxpr/dot_general | solution.py:15
  121.2 2.2 %fusion.36 = f32[8,384,128]{2,1,0:T(8,128)} fusion(f32[8,384,128]{2,1,0:T(8,128)} %get-tuple-element.113, s32[]{:T(128)S(6)} %copy.13, f32[384,1536]{1,0:T(8,128)S(1)} %get-tuple-element.100, f32[384]{0:T(512)S(1)} %broadcast_maximum_fusion.2, bf16[8,1536,128]{2,1,0:T(8,128)(2,1)} %get-tuple-element.124, f32[384]{0:T(512)S(1)} %get-tuple-element.102), kind=kOutput, calls=%fused_computation.8.clone.1 | convolution fusion | flops 152223744 | bytes 2953216 | tf_op jit(solution)/shard_map/while/body/eval_jaxpr/dot_general | solution.py:24
  123.4 1.6 %fusion.34 = (f32[384]{0:T(512)S(1)}, f32[384,1536]{1,0:T(8,128)S(1)}) fusion(bf16[8,1536,128]{2,1,0:T(8,128)(2,1)} %get-tuple-element.123, s32[]{:T(128)S(6)} %copy.13, bf16[8,384,128]{2,1,0:T(8,128)(2,1)} %get-tuple-element.122), kind=kOutput, calls=%fused_computation.28.clone.1 | convolution fusion | flops 152174208 | bytes 2853376 | tf_op jit(solution)/shard_map/while/body/eval_jaxpr/dot_general | solution.py:15
  125.5 2.2 %fusion.36 = f32[8,384,128]{2,1,0:T(8,128)} fusion(f32[8,384,128]{2,1,0:T(8,128)} %get-tuple-element.113, s32[]{:T(128)S(6)} %copy.13, f32[384,1536]{1,0:T(8,128)S(1)} %get-tuple-element.100, f32[384]{0:T(512)S(1)} %broadcast_maximum_fusion.2, bf16[8,1536,128]{2,1,0:T(8,128)(2,1)} %get-tuple-element.124, f32[384]{0:T(512)S(1)} %get-tuple-element.102), kind=kOutput, calls=%fused_computation.8.clone.1 | convolution fusion | flops 152223744 | bytes 2953216 | tf_op jit(solution)/shard_map/while/body/eval_jaxpr/dot_general | solution.py:24
  127.8 1.6 %fusion.34 = (f32[384]{0:T(512)S(1)}, f32[384,1536]{1,0:T(8,128)S(1)}) fusion(bf16[8,1536,128]{2,1,0:T(8,128)(2,1)} %get-tuple-element.123, s32[]{:T(128)S(6)} %copy.13, bf16[8,384,128]{2,1,0:T(8,128)(2,1)} %get-tuple-element.122), kind=kOutput, calls=%fused_computation.28.clone.1 | convolution fusion | flops 152174208 | bytes 2853376 | tf_op jit(solution)/shard_map/while/body/eval_jaxpr/dot_general | solution.py:15
  129.9 2.2 %fusion.36 = f32[8,384,128]{2,1,0:T(8,128)} fusion(f32[8,384,128]{2,1,0:T(8,128)} %get-tuple-element.113, s32[]{:T(128)S(6)} %copy.13, f32[384,1536]{1,0:T(8,128)S(1)} %get-tuple-element.100, f32[384]{0:T(512)S(1)} %broadcast_maximum_fusion.2, bf16[8,1536,128]{2,1,0:T(8,128)(2,1)} %get-tuple-element.124, f32[384]{0:T(512)S(1)} %get-tuple-element.102), kind=kOutput, calls=%fused_computation.8.clone.1 | convolution fusion | flops 152223744 | bytes 2953216 | tf_op jit(solution)/shard_map/while/body/eval_jaxpr/dot_general | solution.py:24
  132.1 1.6 %fusion.34 = (f32[384]{0:T(512)S(1)}, f32[384,1536]{1,0:T(8,128)S(1)}) fusion(bf16[8,1536,128]{2,1,0:T(8,128)(2,1)} %get-tuple-element.123, s32[]{:T(128)S(6)} %copy.13, bf16[8,384,128]{2,1,0:T(8,128)(2,1)} %get-tuple-element.122), kind=kOutput, calls=%fused_computation.28.clone.1 | convolution fusion | flops 152174208 | bytes 2853376 | tf_op jit(solution)/shard_map/while/body/eval_jaxpr/dot_general | solution.py:15
  134.3 2.2 %fusion.36 = f32[8,384,128]{2,1,0:T(8,128)} fusion(f32[8,384,128]{2,1,0:T(8,128)} %get-tuple-element.113, s32[]{:T(128)S(6)} %copy.13, f32[384,1536]{1,0:T(8,128)S(1)} %get-tuple-element.100, f32[384]{0:T(512)S(1)} %broadcast_maximum_fusion.2, bf16[8,1536,128]{2,1,0:T(8,128)(2,1)} %get-tuple-element.124, f32[384]{0:T(512)S(1)} %get-tuple-element.102), kind=kOutput, calls=%fused_computation.8.clone.1 | convolution fusion | flops 152223744 | bytes 2953216 | tf_op jit(solution)/shard_map/while/body/eval_jaxpr/dot_general | solution.py:24
  136.5 5.2 %multiply_reduce_fusion = (f32[384]{0:T(512)S(1)}, f32[384,2048]{1,0:T(8,128)S(1)}) fusion(bf16[8,128,2048]{2,1,0:T(8,128)(2,1)} %param.14, f32[8,384,128]{2,1,0:T(8,128)} %get-tuple-element.38, f32[8,384]{1,0:T(8,128)S(1)} %get-tuple-element.39, bf16[384,2048]{1,0:T(8,128)(2,1)} %param.9), kind=kOutput, calls=%fused_computation.22 | convolution fusion | flops 1614544512 | bytes 10499584 | tf_op jit(solution)/shard_map/hqd,hde->qe/dot_general | solution.py:59
  141.8 1.7 %fusion.23 = bf16[384,2048]{1,0:T(8,128)(2,1)} fusion(bf16[384,2048]{1,0:T(8,128)(2,1)S(1)} %copy-done, f32[384,2048]{1,0:T(8,128)S(1)} %get-tuple-element.57, f32[2048]{0:T(1024)S(1)} %convert_element_type.17, f32[384]{0:T(512)S(1)} %add_rsqrt_fusion, pred[384]{0:T(512)(128)(4,1)S(1)} %broadcast_compare_fusion), kind=kLoop, calls=%fused_computation.23 | loop fusion | flops 3145728 | bytes 6301568 | tf_op jit(solution)/shard_map/jit(_where)/select_n | solution.py:67
  (48 shorter events, 5.1 us)
Async XLA Ops:
  6.5 49.2 %all-gather.3.cloned.1.call-start = ((), (), s32[]{:S(2)}) async-start(), calls=%async_computation | async-start | bytes 3932160 | tf_op jit(solution)/shard_map/all_gather | solution.py:46
  7.3 94.2 %all-gather.5.cloned.1.call-start = ((), (), s32[]{:S(2)}) async-start(), calls=%async_computation.1 | async-start | bytes 3932160 | tf_op jit(solution)/shard_map/all_gather | solution.py:47
  136.5 5.2 %copy-start = (bf16[384,2048]{1,0:T(8,128)(2,1)S(1)}, bf16[384,2048]{1,0:T(8,128)(2,1)}, u32[]{:S(2)}) copy-start(bf16[384,2048]{1,0:T(8,128)(2,1)} %param.9) | copy-start | bytes 4718596
Sparse Core Ops, SparseCore 0:
  9.2 46.5 all-gather.2
  57.6 43.8 all-gather.4
where the time goes:
time: 151 us; the launch traced here: 150 us
  waiting for transfers between devices  93.5 us (62%)
  matrix products  35.8 us (24%)
  between operations  13.4 us (9%)
  other arithmetic  6.97 us (5%)
    all_gather x1, waiting for transfers between devices, attend_keys(): lax.all_gather(key_vectors, 'ctx', axis=1, tiled=True)  46.4 us
    all_gather x1, waiting for transfers between devices, attend_keys(): lax.all_gather(value_vectors, 'ctx', axis=1, tiled=True)  45.7 us
    dot_general x8, matrix products, per_head(): jnp.dot(exponents.astype(jnp.bfloat16), value_head, preferred_element_typ...  17.7 us
    dot_general x8, matrix products, per_head(): lax.dot_general(query_head, key_head, (((1,), (1,)), ((), ())), preferred...  12.8 us
    dot_general x1, matrix products, on_device(): jnp.einsum('hqd,hde->qe', attended, out_weight, preferred_element_type=jn...  5.22 us
    reduce_sum x8, other arithmetic, per_head(): sum_head = sum_head * shrink + jnp.sum(exponents, axis=1)  3.76 us
  transfers between devices with their start and end apart: 2, of which 2 were waited for; matrix products, arithmetic and copies ran while one was open for 1% of the time, Pallas kernels for 0%

commit v1 on v0

--- a/solution.py
+++ b/solution.py
@@ -1,9 +1,253 @@
+import functools
+
 import jax
 import jax.numpy as jnp
 from jax import lax
+from jax.experimental import pallas as pl
+from jax.experimental.pallas import tpu as pltpu
 from jax.sharding import PartitionSpec as P
 
 STEP = 2
+TILE = 128
+LOG2E = 1.4426950408889634
+
+
+def peer_of(me, step, n):
+    peer = 0
+    bit = 1
+    while bit < n:
+        digit = (me // bit) % 2
+        if step & bit:
+            digit = (digit + 1) % 2
+        peer = peer + digit * bit
+        bit *= 2
+    return peer
+
+
+def split_kernel(
+    n,
+    share,
+    q_hbm,
+    k_hbm,
+    v_hbm,
+    flag_hbm,
+    state_hbm,
+    w_hbm,
+    gain_ref,
+    out_ref,
+    q_buf,
+    k_buf,
+    v_buf,
+    flag_buf,
+    state_buf,
+    w_buf,
+    probs,
+    inv_sum,
+    att_buf,
+    update,
+    send_sem,
+    recv_sem,
+    att_send,
+    att_recv,
+    local_sem,
+    big_sem,
+):
+    me = lax.axis_index("ctx")
+    rows, width = q_hbm.shape[1], q_hbm.shape[2]
+    scale = width ** (-0.5) * LOG2E
+    peers = [peer_of(me, step, n) for step in range(n)]
+
+    def mine(ref, device):
+        return ref.at[pl.ds(device * share, share)]
+
+    tensors = ((k_hbm, k_buf), (q_hbm, q_buf), (v_hbm, v_buf))
+    own = []
+    for index, (src, buf) in enumerate(tensors):
+        own.append(pltpu.make_async_copy(mine(src, me), buf.at[me], local_sem.at[index]))
+    own.append(pltpu.make_async_copy(flag_hbm, flag_buf.at[me], local_sem.at[3]))
+    for copy in own:
+        copy.start()
+
+    barrier = pltpu.get_barrier_semaphore()
+    for step in range(1, n):
+        pl.semaphore_signal(
+            barrier, inc=1, device_id={"ctx": peers[step]}, device_id_type=pl.DeviceIdType.MESH
+        )
+    pl.semaphore_wait(barrier, n - 1)
+
+    order = list(range(n - 1, 0, -1))
+
+    def remote(src, dst, send, recv, step):
+        return pltpu.make_async_remote_copy(
+            src_ref=src,
+            dst_ref=dst,
+            send_sem=send,
+            recv_sem=recv,
+            device_id={"ctx": peers[step]},
+            device_id_type=pl.DeviceIdType.MESH,
+        )
+
+    sends = {}
+    for step in order:
+        sends[3, step] = remote(
+            flag_hbm, flag_buf.at[me], send_sem.at[3, step], recv_sem.at[3, step], step
+        )
+        sends[3, step].start()
+    for index, (src, buf) in enumerate(tensors):
+        for step in order:
+            sends[index, step] = remote(
+                mine(src, peers[step]),
+                buf.at[me],
+                send_sem.at[index, step],
+                recv_sem.at[index, step],
+                step,
+            )
+            sends[index, step].start()
+
+    w_copy = pltpu.make_async_copy(w_hbm, w_buf, big_sem.at[0])
+    w_copy.start()
+    state_copy = pltpu.make_async_copy(state_hbm, state_buf, big_sem.at[1])
+    state_copy.start()
+
+    for index in (3, 0, 1):
+        own[index].wait()
+        for step in order:
+            sends[index, step].wait_recv()
+
+    for h in range(share):
+        chosen = None
+        for src in range(n):
+            term = q_buf[src, h].astype(jnp.float32) * flag_buf[src, 0:1, :]
+            chosen = term if chosen is None else chosen + term
+        queries = chosen.astype(jnp.bfloat16)
+        for block in range(rows // TILE):
+            part = queries[block * TILE : (block + 1) * TILE]
+            scores = [
+                lax.dot_general(
+                    part,
+                    k_buf[src, h],
+                    (((1,), (1,)), ((), ())),
+                    preferred_element_type=jnp.float32,
+                )
+                for src in range(n)
+            ]
+            top = jnp.max(scores[0], axis=1, keepdims=True)
+            for piece in scores[1:]:
+                top = jnp.maximum(top, jnp.max(piece, axis=1, keepdims=True))
+            total = None
+            for src, piece in enumerate(scores):
+                weights = jnp.exp2((piece - top) * scale)
+                term = jnp.sum(weights, axis=1, keepdims=True)
+                total = term if total is None else total + term
+                probs[h, src, block * TILE : (block + 1) * TILE, :] = weights.astype(jnp.bfloat16)
+            inv_sum[h, block * TILE : (block + 1) * TILE, :] = jnp.broadcast_to(
+                1.0 / total, (TILE, width)
+            )
+
+    own[2].wait()
+    for step in order:
+        sends[2, step].wait_recv()
+
+    for h in range(share):
+        weighted = None
+        for src in range(n):
+            term = jnp.dot(probs[h, src], v_buf[src, h], preferred_element_type=jnp.float32)
+            weighted = term if weighted is None else weighted + term
+        att_buf[me, :, h * width : (h + 1) * width] = (weighted * inv_sum[h]).astype(jnp.bfloat16)
+
+    att_sends = {}
+    for step in order:
+        att_sends[step] = remote(
+            att_buf.at[me], att_buf.at[me], att_send.at[step], att_recv.at[step], step
+        )
+        att_sends[step].start()
+
+    w_copy.wait()
+    state_copy.wait()
+    span = share * width
+
+    def project(source, first):
+        def body(block, carry):
+            cut = pl.ds(pl.multiple_of(block * TILE, TILE), TILE)
+            weight = w_buf[pl.ds(pl.multiple_of(source * span, span), span), :]
+            product = jnp.dot(att_buf[source, cut, :], weight, preferred_element_type=jnp.float32)
+            if first:
+                update[cut, :] = state_buf[cut, :].astype(jnp.float32) + product
+            else:
+                update[cut, :] = update[cut, :] + product
+            return carry
+
+        lax.fori_loop(0, rows // TILE, body, 0)
+
+    project(me, True)
+    for step in range(1, n):
+        att_sends[step].wait_recv()
+        project(peers[step], False)
+
+    gain = gain_ref[...].astype(jnp.float32)
+    piece_rows = 32
+
+    def finish(block, carry):
+        cut = pl.ds(pl.multiple_of(block * piece_rows, piece_rows), piece_rows)
+        mixed = update[cut, :]
+        mean = jnp.mean(mixed * mixed, axis=-1, keepdims=True)
+        out_ref[cut, :] = (mixed * lax.rsqrt(mean + 1e-06) * gain).astype(out_ref.dtype)
+        return carry
+
+    lax.fori_loop(0, rows // piece_rows, finish, 0)
+
+    for copy in sends.values():
+        copy.wait_send()
+    for copy in att_sends.values():
+        copy.wait_send()
+
+
+def split_heads(n, state_rows, q, k, v, halt_counts, out_weight, norm_gain):
+    heads, rows, width = q.shape
+    share = heads // n
+    features = state_rows.shape[1]
+    flag = jnp.broadcast_to((halt_counts[0] > STEP).astype(jnp.float32), (8, 128))
+    bf16, f32 = jnp.bfloat16, jnp.float32
+    anywhere = pl.BlockSpec(memory_space=pl.ANY)
+    vmem = pl.BlockSpec(memory_space=pltpu.VMEM)
+    block = pltpu.VMEM((n, share, rows, width), bf16)
+    normed = pl.pallas_call(
+        functools.partial(split_kernel, n, share),
+        out_shape=jax.ShapeDtypeStruct((rows, features), bf16),
+        in_specs=[anywhere] * 6 + [vmem],
+        out_specs=vmem,
+        scratch_shapes=[
+            block,
+            block,
+            block,
+            pltpu.VMEM((n, 8, 128), f32),
+            pltpu.VMEM((rows, features), bf16),
+            pltpu.VMEM((heads * width, features), bf16),
+            pltpu.VMEM((share, n, rows, rows), bf16),
+            pltpu.VMEM((share, rows, width), f32),
+            pltpu.VMEM((n, rows, share * width), bf16),
+            pltpu.VMEM((rows, features), f32),
+            pltpu.SemaphoreType.DMA((4, n)),
+            pltpu.SemaphoreType.DMA((4, n)),
+            pltpu.SemaphoreType.DMA((n,)),
+            pltpu.SemaphoreType.DMA((n,)),
+            pltpu.SemaphoreType.DMA((4,)),
+            pltpu.SemaphoreType.DMA((2,)),
+        ],
+        compiler_params=pltpu.CompilerParams(
+            collective_id=0, has_side_effects=True, vmem_limit_bytes=40 * 1024 * 1024
+        ),
+    )(
+        q,
+        k,
+        v,
+        flag,
+        state_rows,
+        out_weight.reshape(heads * width, features),
+        norm_gain.reshape(1, features),
+    )
+    active = (halt_counts > STEP)[:, None]
+    return jnp.where(active, normed, state_rows)
 
 
 def fold_heads(carry, queries, key_piece, value_piece, score_scale):
@@ -68,6 +312,15 @@
 
 
 def solution(mesh):
+    n_ctx = mesh.shape["ctx"]
+
+    def per_device(state_rows, q, k, v, halt_counts, out_weight, norm_gain):
+        heads, rows, _ = q.shape
+        one_owner = rows == (n_ctx - 1) * TILE
+        if one_owner and heads % n_ctx == 0 and n_ctx & (n_ctx - 1) == 0:
+            return split_heads(n_ctx, state_rows, q, k, v, halt_counts, out_weight, norm_gain)
+        return on_device(state_rows, q, k, v, halt_counts, out_weight, norm_gain)
+
     placed = (
         P(("dp", "ctx"), None),
         P(None, ("dp", "ctx"), None),
@@ -78,5 +331,5 @@
         P(),
     )
     return jax.shard_map(
-        on_device, mesh=mesh, in_specs=placed, out_specs=P(("dp", "ctx"), None), check_vma=False
-    )
+        per_device, mesh=mesh, in_specs=placed, out_specs=P(("dp", "ctx"), None), check_vma=False
+    )

time: 151 us -> 57.9 us (0.38)
  waiting for transfers between devices: 93.5 us -> 0 us
  Pallas kernels: 0 us -> 46.6 us
  matrix products: 35.8 us -> 0 us
  between operations: 13.4 us -> 0.7 us
  local copies, waits for them, and re-layouts: 0.46 us -> 8.88 us
  other arithmetic: 6.97 us -> 1.42 us
    all_gather x2 -> x0, waiting for transfers between devices: 92.1 us -> none  [the longest x1 46.4 us: attend_keys(): lax.all_gather(key_vectors, 'ctx', axis=1, tiled=True)]
    pallas_call x0 -> x1, Pallas kernels: none -> 46.6 us  [split_heads(): pl.pallas_call(functools.partial(split_kernel, n, share), out_shape=jax.S...]
    dot_general x17 -> x0, matrix products: 35.8 us -> none  [the longest x8 17.7 us: per_head(): jnp.dot(exponents.astype(jnp.bfloat16), value_head, preferred_element_typ...]
    unnamed x2 -> x12, local copies, waits for them, and re-layouts: 0.01 us -> 6.99 us
    reduce_sum x8 -> x0, other arithmetic: 3.76 us -> none  [per_head(): sum_head = sum_head * shrink + jnp.sum(exponents, axis=1)]
  transfers between devices with their start and end apart: 2 -> 0, of which waited for: 2 -> 0; matrix products, arithmetic and copies ran while one was open for 1% -> 0% of each run, Pallas kernels for 0% -> 0%
where the time goes in v1:
time: 57.9 us; the launch traced here: 57.6 us
  Pallas kernels  46.6 us (80%)
  local copies, waits for them, and re-layouts  8.88 us (15%)
  other arithmetic  1.42 us (2%)
  between operations  0.7 us (1%)
    pallas_call x1, Pallas kernels, split_heads(): pl.pallas_call(functools.partial(split_kernel, n, share), out_shape=jax.S...  46.6 us
    unnamed x12, local copies, waits for them, and re-layouts  6.99 us
    select_n x1, other arithmetic, split_heads(): return jnp.where(active, normed, state_rows)  1.41 us
    slice x1, local copies, waits for them, and re-layouts, split_heads(): halt_counts[0] > STEP  1.19 us

profile of v1, /device:TPU:0, one launch (start us, length us, event | category | flops | bytes accessed | tf_op | source)
XLA Modules:
  0.0 57.6 jit_solution(4267520085125791079)
XLA Ops:
  0.0 0.7 %reshape.12.gain_ref = bf16[1,2048]{1,0:T(2,128)(2,1)S(1)} reshape(bf16[2048]{0:T(1024)(128)(2,1)} %param.13) | data formatting | bytes 8192 | tf_op jit(solution)/shard_map/reshape | solution.py:247
  0.7 1.2 %slice.3 = s32[1]{0:T(128)} slice(s32[384]{0:T(512)} %param.11), slice={[0:1]} | slice | bytes 8 | tf_op jit(solution)/shard_map/slice | solution.py:209
  2.5 0.0 copy-start
  2.6 1.4 %copy-done = bf16[384,2048]{1,0:T(8,128)(2,1)S(1)} copy-done((bf16[384,2048]{1,0:T(8,128)(2,1)S(1)}, bf16[384,2048]{1,0:T(8,128)(2,1)}, u32[]{:S(2)}) %copy-start) | copy-done | bytes 1572888
  4.0 0.0 copy-start.1
  4.0 2.2 %copy-done.1 = bf16[8,128,2048]{2,1,0:T(8,128)(2,1)S(1)} copy-done((bf16[8,128,2048]{2,1,0:T(8,128)(2,1)S(1)}, bf16[8,128,2048]{2,1,0:T(8,128)(2,1)}, u32[]{:S(2)}) %copy-start.1) | copy-done | bytes 4194328
  6.2 0.0 copy-start.2
  6.2 1.1 %copy-done.2 = bf16[8,384,128]{2,1,0:T(8,128)(2,1)S(1)} copy-done((bf16[8,384,128]{2,1,0:T(8,128)(2,1)S(1)}, bf16[8,384,128]{2,1,0:T(8,128)(2,1)}, u32[]{:S(2)}) %copy-start.2) | copy-done | bytes 786456
  7.3 0.0 copy-start.3
  7.3 1.1 %copy-done.3 = bf16[8,384,128]{2,1,0:T(8,128)(2,1)S(1)} copy-done((bf16[8,384,128]{2,1,0:T(8,128)(2,1)S(1)}, bf16[8,384,128]{2,1,0:T(8,128)(2,1)}, u32[]{:S(2)}) %copy-start.3) | copy-done | bytes 786456
  8.4 0.0 copy-start.4
  8.4 1.1 %copy-done.4 = bf16[8,384,128]{2,1,0:T(8,128)(2,1)S(1)} copy-done((bf16[8,384,128]{2,1,0:T(8,128)(2,1)S(1)}, bf16[8,384,128]{2,1,0:T(8,128)(2,1)}, u32[]{:S(2)}) %copy-start.4) | copy-done | bytes 786456
  9.6 0.0 copy-start.5
  9.6 46.6 %shard_map.73 = bf16[384,2048]{1,0:T(8,128)(2,1)S(1)} custom-call(bf16[8,384,128]{2,1,0:T(8,128)(2,1)S(1)} %copy-done.2, bf16[8,384,128]{2,1,0:T(8,128)(2,1)S(1)} %copy-done.3, bf16[8,384,128]{2,1,0:T(8,128)(2,1)S(1)} %copy-done.4, f32[8,128]{1,0:T(8,128)S(1)} %broadcast_in_dim.13.flag_hbm, bf16[384,2048]{1,0:T(8,128)(2,1)S(1)} %copy-done, ...), custom_call_target="tpu_custom_call" | custom-call | tf_op jit(solution)/shard_map/pallas_call | solution.py:214
  56.1 0.0 copy-done.5
  56.2 1.4 %broadcast_select_fusion = bf16[384,2048]{1,0:T(8,128)(2,1)} fusion(bf16[384,2048]{1,0:T(8,128)(2,1)S(1)} %shard_map.73, bf16[384,2048]{1,0:T(8,128)(2,1)S(1)} %copy-done, pred[384]{0:T(512)(128)(4,1)S(1)} %broadcast_compare_fusion), kind=kLoop, calls=%fused_computation | loop fusion | flops 786432 | bytes 4718976 | tf_op jit(solution)/shard_map/jit(_where)/select_n | solution.py:250
  (2 shorter events, 0.0 us)
Async XLA Ops:
  2.5 1.4 %copy-start = (bf16[384,2048]{1,0:T(8,128)(2,1)S(1)}, bf16[384,2048]{1,0:T(8,128)(2,1)}, u32[]{:S(2)}) copy-start(bf16[384,2048]{1,0:T(8,128)(2,1)} %state_hbm.1) | copy-start | bytes 4718596
  4.0 2.2 %copy-start.1 = (bf16[8,128,2048]{2,1,0:T(8,128)(2,1)S(1)}, bf16[8,128,2048]{2,1,0:T(8,128)(2,1)}, u32[]{:S(2)}) copy-start(bf16[8,128,2048]{2,1,0:T(8,128)(2,1)} %param.12) | copy-start | bytes 12582916
  6.2 1.1 %copy-start.2 = (bf16[8,384,128]{2,1,0:T(8,128)(2,1)S(1)}, bf16[8,384,128]{2,1,0:T(8,128)(2,1)}, u32[]{:S(2)}) copy-start(bf16[8,384,128]{2,1,0:T(8,128)(2,1)} %q_hbm.1) | copy-start | bytes 2359300
  7.3 1.1 %copy-start.3 = (bf16[8,384,128]{2,1,0:T(8,128)(2,1)S(1)}, bf16[8,384,128]{2,1,0:T(8,128)(2,1)}, u32[]{:S(2)}) copy-start(bf16[8,384,128]{2,1,0:T(8,128)(2,1)} %k_hbm.1) | copy-start | bytes 2359300
  8.4 1.1 %copy-start.4 = (bf16[8,384,128]{2,1,0:T(8,128)(2,1)S(1)}, bf16[8,384,128]{2,1,0:T(8,128)(2,1)}, u32[]{:S(2)}) copy-start(bf16[8,384,128]{2,1,0:T(8,128)(2,1)} %v_hbm.1) | copy-start | bytes 2359300
  9.6 46.6 %copy-start.5 = (s32[384]{0:T(512)S(1)}, s32[384]{0:T(512)}, u32[]{:S(2)}) copy-start(s32[384]{0:T(512)} %param.11) | copy-start | bytes 4612

commit v2 on v0

--- a/solution.py
+++ b/solution.py
@@ -1,9 +1,263 @@
+import functools
+
 import jax
 import jax.numpy as jnp
 from jax import lax
+from jax.experimental import pallas as pl
+from jax.experimental.pallas import tpu as pltpu
 from jax.sharding import PartitionSpec as P
 
 STEP = 2
+TILE = 128
+LOG2E = 1.4426950408889634
+
+
+def peer_of(me, step, n):
+    peer = 0
+    bit = 1
+    while bit < n:
+        digit = (me // bit) % 2
+        if step & bit:
+            digit = (digit + 1) % 2
+        peer = peer + digit * bit
+        bit *= 2
+    return peer
+
+
+def split_kernel(
+    n,
+    share,
+    halt_ref,
+    q_hbm,
+    k_hbm,
+    v_hbm,
+    state_hbm,
+    w_hbm,
+    gain_ref,
+    out_ref,
+    q_buf,
+    k_buf,
+    v_buf,
+    flag_out,
+    flag_buf,
+    state_buf,
+    w_buf,
+    probs,
+    inv_sum,
+    att_buf,
+    update,
+    send_sem,
+    recv_sem,
+    flag_send,
+    flag_recv,
+    att_send,
+    att_recv,
+    local_sem,
+    w_sem,
+    state_sem,
+):
+    me = lax.axis_index("ctx")
+    rows, width = q_hbm.shape[1], q_hbm.shape[2]
+    blocks = rows // TILE
+    scale = width ** (-0.5) * LOG2E
+    peers = [peer_of(me, step, n) for step in range(n)]
+    order = list(range(n - 1, 0, -1))
+    tensors = ((k_hbm, k_buf), (q_hbm, q_buf), (v_hbm, v_buf))
+    own_rows = pl.ds(pl.multiple_of(me * rows, rows), rows)
+    own_lanes = pl.ds(pl.multiple_of(me * width, width), width)
+
+    flag = jnp.full(flag_out.shape, halt_ref[0] > STEP).astype(jnp.float32)
+    flag_out[...] = flag
+
+    own = {}
+    for h in range(share):
+        for index, (src, buf) in enumerate(tensors):
+            own[index, h] = pltpu.make_async_copy(
+                src.at[me * share + h], buf.at[h, own_rows], local_sem.at[index, h]
+            )
+            own[index, h].start()
+
+    barrier = pltpu.get_barrier_semaphore()
+    for step in range(1, n):
+        pl.semaphore_signal(
+            barrier, inc=1, device_id={"ctx": peers[step]}, device_id_type=pl.DeviceIdType.MESH
+        )
+    pl.semaphore_wait(barrier, n - 1)
+
+    def remote(src, dst, send, recv, step):
+        copy = pltpu.make_async_remote_copy(
+            src_ref=src,
+            dst_ref=dst,
+            send_sem=send,
+            recv_sem=recv,
+            device_id={"ctx": peers[step]},
+            device_id_type=pl.DeviceIdType.MESH,
+        )
+        copy.start()
+        return copy
+
+    sends, flags, gathers = {}, {}, {}
+    for h in range(share):
+        for index, (src, buf) in enumerate(tensors):
+            for step in order:
+                sends[index, h, step] = remote(
+                    src.at[peers[step] * share + h],
+                    buf.at[h, own_rows],
+                    send_sem.at[index, h, step],
+                    recv_sem.at[index, h, step],
+                    step,
+                )
+            if h == 0 and index == 0:
+                for step in order:
+                    flags[step] = remote(
+                        flag_out, flag_buf.at[me], flag_send.at[step], flag_recv.at[step], step
+                    )
+
+    w_copies = []
+    for head in range(n * share):
+        w_copies.append(
+            pltpu.make_async_copy(
+                w_hbm.at[head],
+                w_buf.at[head % share, pl.ds((head // share) * width, width)],
+                w_sem.at[head],
+            )
+        )
+        w_copies[-1].start()
+    state_copy = pltpu.make_async_copy(state_hbm, state_buf, state_sem)
+    state_copy.start()
+
+    def arrived(index, h):
+        own[index, h].wait()
+        for step in order:
+            sends[index, h, step].wait_recv()
+
+    def gather(h, block):
+        if block is None:
+            cut, slot = pl.ds(0, rows), 0
+        else:
+            cut, slot = pl.ds(block * TILE, TILE), block
+        for step in order:
+            gathers[h, slot, step] = remote(
+                att_buf.at[h, cut, own_lanes],
+                att_buf.at[h, cut, own_lanes],
+                att_send.at[h, slot, step],
+                att_recv.at[h, slot, step],
+                step,
+            )
+
+    for h in range(share):
+        arrived(0, h)
+        arrived(1, h)
+        if h == 0:
+            for step in order:
+                flags[step].wait_recv()
+        for block in range(blocks):
+            base = block * TILE
+            chosen = q_buf[h, pl.ds(pl.multiple_of(me * rows, rows) + base, TILE), :].astype(jnp.float32) * flag[0:1, :]
+            for step in order:
+                start = pl.multiple_of(peers[step] * rows, rows) + base
+                term = q_buf[h, pl.ds(start, TILE), :].astype(jnp.float32)
+                chosen = chosen + term * flag_buf[peers[step], 0:1, :]
+            scores = lax.dot_general(
+                chosen.astype(jnp.bfloat16),
+                k_buf[h],
+                (((1,), (1,)), ((), ())),
+                preferred_element_type=jnp.float32,
+            )
+            top = jnp.max(scores, axis=1, keepdims=True)
+            weights = jnp.exp2((scores - top) * scale)
+            total = jnp.sum(weights, axis=1, keepdims=True)
+            probs[base : base + TILE, :] = weights.astype(jnp.bfloat16)
+            inv_sum[base : base + TILE, :] = jnp.broadcast_to(1.0 / total, (TILE, width))
+        arrived(2, h)
+        last = h == share - 1
+        for block in range(blocks):
+            cut = slice(block * TILE, (block + 1) * TILE)
+            weighted = jnp.dot(probs[cut, :], v_buf[h], preferred_element_type=jnp.float32)
+            att_buf[h, cut, own_lanes] = (weighted * inv_sum[cut, :]).astype(jnp.bfloat16)
+            if last:
+                gather(h, block)
+        if not last:
+            gather(h, None)
+
+    for copy in w_copies:
+        copy.wait()
+    state_copy.wait()
+
+    for h in range(share - 1):
+        for step in order:
+            gathers[h, 0, step].wait_recv()
+
+        def body(block, carry, h=h):
+            cut = pl.ds(pl.multiple_of(block * TILE, TILE), TILE)
+            product = jnp.dot(att_buf[h, cut, :], w_buf[h], preferred_element_type=jnp.float32)
+            if h == 0:
+                update[cut, :] = state_buf[cut, :].astype(jnp.float32) + product
+            else:
+                update[cut, :] = update[cut, :] + product
+            return carry
+
+        lax.fori_loop(0, blocks, body, 0)
+
+    gain = gain_ref[...].astype(jnp.float32).reshape(1, -1)
+    h = share - 1
+    for block in range(blocks):
+        for step in order:
+            gathers[h, block, step].wait_recv()
+        cut = slice(block * TILE, (block + 1) * TILE)
+        mixed = jnp.dot(att_buf[h, cut, :], w_buf[h], preferred_element_type=jnp.float32)
+        residual = update if share > 1 else state_buf
+        mixed = residual[cut, :].astype(jnp.float32) + mixed
+        mean = jnp.mean(mixed * mixed, axis=-1, keepdims=True)
+        out_ref[cut, :] = (mixed * lax.rsqrt(mean + 1e-06) * gain).astype(out_ref.dtype)
+
+    for group in (sends, flags, gathers):
+        for copy in group.values():
+            copy.wait_send()
+
+
+def split_heads(n, state_rows, q, k, v, halt_counts, out_weight, norm_gain):
+    heads, rows, width = q.shape
+    share = heads // n
+    features = state_rows.shape[1]
+    bf16, f32 = jnp.bfloat16, jnp.float32
+    hbm = pl.BlockSpec(memory_space=pltpu.MemorySpace.HBM)
+    vmem = pl.BlockSpec(memory_space=pltpu.VMEM)
+    block = pltpu.VMEM((share, n * rows, width), bf16)
+    dma = pltpu.SemaphoreType.DMA
+    normed = pl.pallas_call(
+        functools.partial(split_kernel, n, share),
+        out_shape=jax.ShapeDtypeStruct((rows, features), bf16),
+        in_specs=[pl.BlockSpec(memory_space=pltpu.SMEM)] + [hbm] * 5 + [vmem],
+        out_specs=vmem,
+        scratch_shapes=[
+            block,
+            block,
+            block,
+            pltpu.VMEM((8, 128), f32),
+            pltpu.VMEM((n, 8, 128), f32),
+            pltpu.VMEM((rows, features), bf16),
+            pltpu.VMEM((share, n * width, features), bf16),
+            pltpu.VMEM((rows, n * rows), bf16),
+            pltpu.VMEM((rows, width), f32),
+            pltpu.VMEM((share, rows, n * width), bf16),
+            pltpu.VMEM((rows, features), f32),
+            dma((3, share, n)),
+            dma((3, share, n)),
+            dma((n,)),
+            dma((n,)),
+            dma((share, rows // TILE, n)),
+            dma((share, rows // TILE, n)),
+            dma((3, share)),
+            dma((heads,)),
+            dma,
+        ],
+        compiler_params=pltpu.CompilerParams(
+            collective_id=0, has_side_effects=True, vmem_limit_bytes=60 * 1024 * 1024
+        ),
+    )(halt_counts, q, k, v, state_rows, out_weight, norm_gain)
+    active = (halt_counts > STEP)[:, None]
+    return jnp.where(active, normed, state_rows)
 
 
 def fold_heads(carry, queries, key_piece, value_piece, score_scale):
@@ -68,6 +322,15 @@
 
 
 def solution(mesh):
+    n_ctx = mesh.shape["ctx"]
+
+    def per_device(state_rows, q, k, v, halt_counts, out_weight, norm_gain):
+        heads, rows, _ = q.shape
+        one_owner = rows == (n_ctx - 1) * TILE
+        if one_owner and heads % n_ctx == 0 and n_ctx & (n_ctx - 1) == 0:
+            return split_heads(n_ctx, state_rows, q, k, v, halt_counts, out_weight, norm_gain)
+        return on_device(state_rows, q, k, v, halt_counts, out_weight, norm_gain)
+
     placed = (
         P(("dp", "ctx"), None),
         P(None, ("dp", "ctx"), None),
@@ -78,5 +341,5 @@
         P(),
     )
     return jax.shard_map(
-        on_device, mesh=mesh, in_specs=placed, out_specs=P(("dp", "ctx"), None), check_vma=False
-    )
+        per_device, mesh=mesh, in_specs=placed, out_specs=P(("dp", "ctx"), None), check_vma=False
+    )

time: 151 us -> 46.4 us (0.31)
  waiting for transfers between devices: 93.5 us -> 0 us
  Pallas kernels: 0 us -> 42.7 us
  matrix products: 35.8 us -> 0 us
  between operations: 13.4 us -> 0.02 us
  other arithmetic: 6.97 us -> 3.46 us
    all_gather x2 -> x0, waiting for transfers between devices: 92.1 us -> none  [the longest x1 46.4 us: attend_keys(): lax.all_gather(key_vectors, 'ctx', axis=1, tiled=True)]
    pallas_call x0 -> x1, Pallas kernels: none -> 42.7 us  [split_heads(): pl.pallas_call(functools.partial(split_kernel, n, share), out_shape=jax.S...]
    dot_general x17 -> x0, matrix products: 35.8 us -> none  [the longest x8 17.7 us: per_head(): jnp.dot(exponents.astype(jnp.bfloat16), value_head, preferred_element_typ...]
    reduce_sum x8 -> x0, other arithmetic: 3.76 us -> none  [per_head(): sum_head = sum_head * shrink + jnp.sum(exponents, axis=1)]
  transfers between devices with their start and end apart: 2 -> 0, of which waited for: 2 -> 0; matrix products, arithmetic and copies ran while one was open for 1% -> 0% of each run, Pallas kernels for 0% -> 0%
where the time goes in v2:
time: 46.4 us; the launch traced here: 46.2 us
  Pallas kernels  42.7 us (92%)
  other arithmetic  3.46 us (7%)
    pallas_call x1, Pallas kernels, split_heads(): pl.pallas_call(functools.partial(split_kernel, n, share), out_shape=jax.S...  42.7 us
    select_n x1, other arithmetic, split_heads(): return jnp.where(active, normed, state_rows)  2.78 us

profile of v2, /device:TPU:0, one launch (start us, length us, event | category | flops | bytes accessed | tf_op | source)
XLA Modules:
  0.0 46.2 jit_solution(7123393658871470632)
XLA Ops:
  0.0 0.7 %broadcast_compare_fusion = pred[384]{0:T(512)(128)(4,1)S(1)} fusion(s32[384]{0:T(512)} %halt_ref.1), kind=kLoop, calls=%fused_computation.1 | loop fusion | flops 384 | bytes 1920 | tf_op jit(solution)/shard_map/gt | solution.py:259
  0.7 0.0 copy-start
  0.7 42.7 %shard_map.73 = bf16[384,2048]{1,0:T(8,128)(2,1)} custom-call(s32[384]{0:T(512)} %halt_ref.1, bf16[8,384,128]{2,1,0:T(8,128)(2,1)} %q_hbm.1, bf16[8,384,128]{2,1,0:T(8,128)(2,1)} %k_hbm.1, bf16[8,384,128]{2,1,0:T(8,128)(2,1)} %v_hbm.1, bf16[384,2048]{1,0:T(8,128)(2,1)} %state_hbm.1, bf16[8,128,2048]{2,1,0:T(8,128)(2,1)} %w_hbm.1, bf16[2048]{0:T(1024)(128)(2,1)} %gain_ref.1), custom_call_target="tpu_custom_call" | custom-call | tf_op jit(solution)/shard_map/pallas_call | solution.py:228
  43.4 0.0 copy-done
  43.4 2.8 %broadcast_select_fusion = bf16[384,2048]{1,0:T(8,128)(2,1)} fusion(bf16[384,2048]{1,0:T(8,128)(2,1)} %shard_map.73, bf16[384,2048]{1,0:T(8,128)(2,1)S(1)} %copy-done, pred[384]{0:T(512)(128)(4,1)S(1)} %broadcast_compare_fusion), kind=kLoop, calls=%fused_computation | loop fusion | flops 786432 | bytes 4718976 | tf_op jit(solution)/shard_map/jit(_where)/select_n | solution.py:260
Async XLA Ops:
  0.7 42.8 %copy-start = (bf16[384,2048]{1,0:T(8,128)(2,1)S(1)}, bf16[384,2048]{1,0:T(8,128)(2,1)}, u32[]{:S(2)}) copy-start(bf16[384,2048]{1,0:T(8,128)(2,1)} %state_hbm.1) | copy-start | bytes 4718596

commit v3 on v2

--- a/solution.py
+++ b/solution.py
@@ -209,7 +209,10 @@
         residual = update if share > 1 else state_buf
         mixed = residual[cut, :].astype(jnp.float32) + mixed
         mean = jnp.mean(mixed * mixed, axis=-1, keepdims=True)
-        out_ref[cut, :] = (mixed * lax.rsqrt(mean + 1e-06) * gain).astype(out_ref.dtype)
+        normed = mixed * lax.rsqrt(mean + 1e-06) * gain
+        active = jnp.full(normed.shape, halt_ref[block * TILE] > STEP)
+        kept = state_buf[cut, :].astype(jnp.float32)
+        out_ref[cut, :] = jnp.where(active, normed, kept).astype(out_ref.dtype)
 
     for group in (sends, flags, gathers):
         for copy in group.values():
@@ -225,7 +228,7 @@
     vmem = pl.BlockSpec(memory_space=pltpu.VMEM)
     block = pltpu.VMEM((share, n * rows, width), bf16)
     dma = pltpu.SemaphoreType.DMA
-    normed = pl.pallas_call(
+    new_state = pl.pallas_call(
         functools.partial(split_kernel, n, share),
         out_shape=jax.ShapeDtypeStruct((rows, features), bf16),
         in_specs=[pl.BlockSpec(memory_space=pltpu.SMEM)] + [hbm] * 5 + [vmem],
@@ -256,8 +259,7 @@
             collective_id=0, has_side_effects=True, vmem_limit_bytes=60 * 1024 * 1024
         ),
     )(halt_counts, q, k, v, state_rows, out_weight, norm_gain)
-    active = (halt_counts > STEP)[:, None]
-    return jnp.where(active, normed, state_rows)
+    return new_state
 
 
 def fold_heads(carry, queries, key_piece, value_piece, score_scale):

time: 46.4 us -> 45.6 us (0.983)
  other arithmetic: 3.46 us -> 0 us
  local copies, waits for them, and re-layouts: 0.01 us -> 2.73 us
    select_n x1 -> x0, other arithmetic: 2.78 us -> none  [split_heads(): return jnp.where(active, normed, state_rows)]
    unnamed x2 -> x1, local copies, waits for them, and re-layouts: 0.01 us -> 2.73 us
    gt x1 -> x0, other arithmetic: 0.69 us -> none  [split_heads(): active = (halt_counts > STEP)[:, None]]
where the time goes in v3:
time: 45.6 us; the launch traced here: 45.4 us
  Pallas kernels  42.7 us (94%)
  local copies, waits for them, and re-layouts  2.73 us (6%)
    pallas_call x1, Pallas kernels, split_heads(): pl.pallas_call(functools.partial(split_kernel, n, share), out_shape=jax.S...  42.7 us
    unnamed x1, local copies, waits for them, and re-layouts  2.73 us

profile of v3, /device:TPU:0, one launch (start us, length us, event | category | flops | bytes accessed | tf_op | source)
XLA Modules:
  0.0 45.4 jit_solution(11139045484995256700)
XLA Ops:
  0.0 42.7 %shard_map.73 = bf16[384,2048]{1,0:T(8,128)(2,1)} custom-call(s32[384]{0:T(512)} %halt_ref.1, bf16[8,384,128]{2,1,0:T(8,128)(2,1)} %q_hbm.1, bf16[8,384,128]{2,1,0:T(8,128)(2,1)} %k_hbm.1, bf16[8,384,128]{2,1,0:T(8,128)(2,1)} %v_hbm.1, bf16[384,2048]{1,0:T(8,128)(2,1)} %state_hbm.1, bf16[8,128,2048]{2,1,0:T(8,128)(2,1)} %w_hbm.1, bf16[2048]{0:T(1024)(128)(2,1)} %gain_ref.1), custom_call_target="tpu_custom_call" | custom-call | tf_op jit(solution)/shard_map/pallas_call | solution.py:231
  42.7 2.7 %copy.9 = bf16[384,2048]{1,0:T(8,128)(2,1)} copy(bf16[384,2048]{1,0:T(8,128)(2,1)} %shard_map.73) | data formatting | bytes 3145728
